TPU v7x, 32 devices: a whole 2x2x4 slice. The times are simulated.
32 devices in a mesh: dp: 4 (over y, core), expert: 4 (over z), tensor: 2 (over x).
Axes of the slice: x: 2, y: 2, z: 4, core: 2. Of those that a mesh axis runs over, the one named last changes fastest.
Arguments:
- router_input: bfloat16 [1024, 2048], P(('dp', 'expert'), 'tensor'), may hold values from -6 to 6
- router_weight: bfloat16 [2048, 8], replicated, may hold values from -0.125 to 0.125
- expert_ids: int32 [1024, 2], P(('dp', 'expert', 'tensor')), may hold values from 0 to 7, all different within a row; in each aligned block of 32 rows (0 to 31, 32 to 63, ...) at most 9 rows name the same one
- down_weight: bfloat16 [61440, 2048], P(('expert', 'tensor')), may hold values from -0.0625 to 0.0625
- hidden: bfloat16 [4, 72, 61440], P('dp', None, ('expert', 'tensor')), may hold values from -6 to 6
- grad_output: bfloat16 [1024, 2048], P(('dp', 'expert', 'tensor')), may hold values from -4 to 4
Outputs:
- weight_grad: bfloat16 [61440, 2048], P(('expert', 'tensor', 'dp'))
- hidden_grad: bfloat16 [4, 72, 61440], P('dp', None, ('expert', 'tensor'))
- router_grad: float32 [2048, 8], replicated
- input_grad: bfloat16 [1024, 2048], P(('dp', 'expert', 'tensor'))
Inputs may be any that keep to these rules, and one draw needn't show every extreme that they name: `expert_ids`: each row names 2 different experts. Within the 32 rows of one device no expert is named more than 9 times, and some device's rows name some expert exactly 9 times.
All inputs are finite; a program needn't handle non-finite values.
Results may differ from a plain program's by a relative error of at most 0.018.
Values may be sent and summed in bfloat16 or wider, within the bound.
No kernel may reach another device: no remote copies, remote signals or barrier semaphores. Data moves between devices by JAX's collectives and lax.ppermute only.
A program may use at most 192 MiB of HBM per device.

v0:
```python
import jax
import jax.numpy as jnp
from jax import lax
from jax.sharding import PartitionSpec as P


def per_device(router_input, router_weight, expert_ids, down_weight, hidden, grad_output):
    token_rows = grad_output.shape[0]
    model_width = grad_output.shape[1]
    expert_count = router_weight.shape[1]
    choose_count = expert_ids.shape[1]
    expert_ranks = lax.axis_size("expert")
    tensor_ranks = lax.axis_size("tensor")
    sources = expert_ranks * tensor_ranks
    spread = sources // expert_count
    capacity = hidden.shape[1] // sources
    full_input = lax.all_to_all(router_input, "tensor", split_axis=0, concat_axis=1, tiled=True)
    logits = jnp.dot(full_input, router_weight, preferred_element_type=jnp.float32)
    labels = jnp.arange(expert_count, dtype=jnp.int32)
    onehot_int = (expert_ids[:, :, None] == labels).astype(jnp.int32)
    onehot = onehot_int.astype(jnp.float32)
    picked = jnp.sum(onehot * logits[:, None, :], axis=2)
    first_gate = jax.nn.sigmoid(picked[:, 0] - picked[:, 1])
    second_gate = jax.nn.sigmoid(picked[:, 1] - picked[:, 0])
    gate_values = jnp.stack([first_gate, second_gate], axis=1)
    gate_low = gate_values.astype(jnp.bfloat16)
    flat_hits = onehot_int.reshape(token_rows * choose_count, expert_count)
    before = jnp.cumsum(flat_hits, axis=0) - flat_hits
    slot_pos = jnp.sum(before * flat_hits, axis=1).reshape(token_rows, choose_count)
    slot_ids = jnp.arange(capacity, dtype=jnp.int32)
    dispatch_table = onehot[:, :, :, None] * (slot_pos[:, :, None, None] == slot_ids).astype(
        jnp.float32
    )
    slot_table = jnp.sum(dispatch_table, axis=1).astype(jnp.bfloat16)
    packed_grad = jnp.einsum(
        "rec,rd->ecd", slot_table, grad_output, preferred_element_type=jnp.float32
    ).astype(jnp.bfloat16)
    packed_gate = jnp.einsum("rkec,rk->ec", dispatch_table, gate_low.astype(jnp.float32)).astype(
        jnp.bfloat16
    )
    send_grad = jnp.repeat(packed_grad, spread, axis=0)
    send_gate = jnp.repeat(packed_gate, spread, axis=0)
    recv_grad, recv_gate = (
        lax.all_to_all(send_grad, ("expert", "tensor"), split_axis=0, concat_axis=0, tiled=True),
        lax.all_to_all(send_gate, ("expert", "tensor"), split_axis=0, concat_axis=0, tiled=True),
    )
    recv_grad = recv_grad.reshape(sources * capacity, model_width)
    recv_gate = recv_gate.reshape(sources * capacity).astype(jnp.float32)
    hidden_rows = hidden[0]
    gated_grad = (recv_gate[:, None] * recv_grad.astype(jnp.float32)).astype(jnp.bfloat16)
    expert_image = lax.dot_general(
        recv_grad, down_weight, (((1,), (1,)), ((), ())), preferred_element_type=jnp.float32
    )
    hidden_part = (recv_gate[:, None] * expert_image).astype(jnp.bfloat16)
    gate_partial = jnp.sum(hidden_rows.astype(jnp.float32) * expert_image, axis=1).reshape(
        sources, capacity
    )
    returned = lax.all_to_all(
        gate_partial, ("expert", "tensor"), split_axis=0, concat_axis=0, tiled=True
    )
    expert_sums = jnp.sum(returned.reshape(expert_count, spread, capacity), axis=1)
    gate_grad = jnp.einsum("rkec,ec->rk", dispatch_table, expert_sums)
    mixed_term = jnp.sum(gate_values * gate_grad, axis=1, keepdims=True)
    logit_part = gate_values * (gate_grad - mixed_term)
    logit_grad = jnp.sum(onehot * logit_part[:, :, None], axis=1)
    input_grad = jnp.dot(
        logit_grad, router_weight.astype(jnp.float32).T, precision=lax.Precision.HIGHEST
    ).astype(jnp.bfloat16)
    router_local = jnp.dot(
        full_input.astype(jnp.float32).T, logit_grad, precision=lax.Precision.HIGHEST
    )
    router_grad = lax.psum(router_local, ("dp", "expert", "tensor"))
    weight_sum = lax.psum_scatter(
        lax.dot_general(
            hidden_rows, gated_grad, (((0,), (0,)), ((), ())), preferred_element_type=jnp.float32
        ).astype(jnp.bfloat16),
        "dp",
        scatter_dimension=0,
        tiled=True,
    )
    return (weight_sum, hidden_part[None], router_grad, input_grad)


def solution(mesh):
    return jax.shard_map(
        per_device,
        mesh=mesh,
        in_specs=(
            P(("dp", "expert"), "tensor"),
            P(),
            P(("dp", "expert", "tensor"), None),
            P(("expert", "tensor"), None),
            P("dp", None, ("expert", "tensor")),
            P(("dp", "expert", "tensor"), None),
        ),
        out_specs=(
            P(("expert", "tensor", "dp"), None),
            P("dp", None, ("expert", "tensor")),
            P(),
            P(("dp", "expert", "tensor"), None),
        ),
        check_vma=False,
    )
```

profile of v0, /device:TPU:0, one launch (start us, length us, event | category | flops | bytes accessed | tf_op | source)
XLA Modules:
  0.0 359.2 jit_solution(10456292851233868904)
XLA Ops:
  8.0 4.4 %all-to-all-start = ((bf16[2,32,1024]{2,1,0:T(8,128)(2,1)}), bf16[2,32,1024]{2,1,0:T(8,128)(2,1)S(1)}, u32[]{:S(2)}, u32[]{:S(2)}) async-start(bf16[2,32,1024]{2,1,0:T(8,128)(2,1)} %bitcast.52), calls=%async_computation | async-start | bytes 262144 | tf_op jit(solution)/shard_map/all_to_all | solution.py:17
  12.4 0.8 copy.28
  13.2 0.7 convert_convert_fusion
  14.5 2.4 all-to-all-done
  17.0 0.9 fusion.15
  17.9 0.7 multiply_reduce_fusion.3
  18.9 0.6 copy.31
  19.5 5.4 %all-to-all-start.1 = ((bf16[8,1,9]{2,1,0:T(2,128)(2,1)}), bf16[8,1,9]{2,1,0:T(2,128)(2,1)S(1)}, u32[]{:S(2)}, u32[]{:S(2)}) async-start(bf16[8,1,9]{2,1,0:T(2,128)(2,1)} %copy.31), calls=%async_computation.1 | async-start | bytes 8192 | tf_op jit(solution)/shard_map/all_to_all | solution.py:45
  24.9 1.1 convolution_convert_fusion
  26.0 5.3 %all-to-all-done.1 = bf16[8,1,9]{2,1,0:T(2,128)(2,1)S(1)} async-done(((bf16[8,1,9]{2,1,0:T(2,128)(2,1)}), bf16[8,1,9]{2,1,0:T(2,128)(2,1)S(1)}, u32[]{:S(2)}, u32[]{:S(2)}) %all-to-all-start.1) | async-done | bytes 176 | tf_op jit(solution)/shard_map/all_to_all | solution.py:45
  31.3 3.5 all-to-all-start.2
  34.9 12.0 %all-to-all-done.2 = bf16[8,9,2048]{2,1,0:T(8,128)(2,1)S(1)} async-done(((bf16[8,9,2048]{2,1,0:T(8,128)(2,1)}), bf16[8,9,2048]{2,1,0:T(8,128)(2,1)S(1)}, u32[]{:S(2)}, u32[]{:S(2)}) %all-to-all-start.2) | async-done | bytes 294944 | tf_op jit(solution)/shard_map/all_to_all | solution.py:44
  47.1 15.5 %multiply_reduce_fusion = (f32[72]{0:T(128)S(1)}, bf16[1,72,7680]{2,1,0:T(8,128)(2,1)}) fusion(bf16[1,72,7680]{2,1,0:T(8,128)(2,1)S(1)} %copy-done.2, f32[72]{0:T(128)S(1)} %reshape.65, bf16[72,2048]{1,0:T(8,128)(2,1)S(1)} %reshape.63, bf16[7680,2048]{1,0:T(8,128)(2,1)} %param.9), kind=kOutput, calls=%fused_computation.4 | convolution fusion | flops 2267688960 | bytes 33964608 | tf_op jit(solution)/shard_map/dot_general | solution.py:51
  62.6 0.7 all_to_all.36
  63.3 3.7 %all-to-all-start.3 = ((f32[8,1,9]{2,1,0:T(1,128)}), f32[8,1,9]{2,1,0:T(1,128)S(1)}, u32[]{:S(2)}, u32[]{:S(2)}) async-start(f32[8,1,9]{2,1,0:T(1,128)} %bitcast.12), calls=%async_computation.3 | async-start | bytes 8192 | tf_op jit(solution)/shard_map/all_to_all | solution.py:58
  67.3 6.1 %all-to-all-done.3 = f32[8,1,9]{2,1,0:T(1,128)S(1)} async-done(((f32[8,1,9]{2,1,0:T(1,128)}), f32[8,1,9]{2,1,0:T(1,128)S(1)}, u32[]{:S(2)}, u32[]{:S(2)}) %all-to-all-start.3) | async-done | bytes 320 | tf_op jit(solution)/shard_map/all_to_all | solution.py:58
  73.6 0.8 convolution_bitcast_fusion
  74.5 13.9 %convert_bitcast_fusion = bf16[7680,2048]{0,1:T(8,128)(2,1)} fusion(bf16[72,2048]{1,0:T(8,128)(2,1)S(1)} %convert_element_type.93, bf16[1,72,7680]{2,1,0:T(8,128)(2,1)S(1)} %copy-done.2), kind=kOutput, calls=%fused_computation | convolution fusion | flops 2280652800 | bytes 32858112 | tf_op jit(solution)/shard_map/dot_general | solution.py:74
  88.4 40.7 %copy.43 = bf16[7680,2048]{1,0:T(8,128)(2,1)} copy(bf16[7680,2048]{0,1:T(8,128)(2,1)} %convert_bitcast_fusion) | data formatting | bytes 62914560
  129.1 0.7 copy-done.3
  129.8 1.0 convolution_convert_fusion.1
  130.8 159.6 %all-reduce.2.cloned.1.call-done = f32[2048,8]{0,1:T(8,128)} async-done(((f32[2048,8]{0,1:T(8,128)}), f32[2048,8]{0,1:T(8,128)}) %all-reduce.2.cloned.1.call-update) | async-done | bytes 65552 | tf_op jit(solution)/shard_map/psum | solution.py:72
  290.4 59.9 %reduce-scatter.4.cloned.1.call-done = bf16[1920,2048]{1,0:T(8,128)(2,1)} async-done(((bf16[7680,2048]{1,0:T(8,128)(2,1)}), bf16[1920,2048]{1,0:T(8,128)(2,1)}) %reduce-scatter.4.cloned.1.call-update) | async-done | bytes 7864336
  350.2 1.5 copy.55
  (37 shorter events, 1.9 us)
Async XLA Ops:
  8.0 16.9 %copy-start = (bf16[32,2048]{1,0:T(8,128)(2,1)S(1)}, bf16[32,2048]{1,0:T(8,128)(2,1)}, u32[]{:S(2)}) copy-start(bf16[32,2048]{1,0:T(8,128)(2,1)} %param.11) | copy-start | bytes 393220
  8.0 39.1 %copy-start.2 = (bf16[1,72,7680]{2,1,0:T(8,128)(2,1)S(1)}, bf16[1,72,7680]{2,1,0:T(8,128)(2,1)}, u32[]{:S(2)}) copy-start(bf16[1,72,7680]{2,1,0:T(8,128)(2,1)} %param.10) | copy-start | bytes 3317764
  8.0 8.9 %all-to-all-start = ((bf16[2,32,1024]{2,1,0:T(8,128)(2,1)}), bf16[2,32,1024]{2,1,0:T(8,128)(2,1)S(1)}, u32[]{:S(2)}, u32[]{:S(2)}) async-start(bf16[2,32,1024]{2,1,0:T(8,128)(2,1)} %bitcast.52), calls=%async_computation | async-start | bytes 262144 | tf_op jit(solution)/shard_map/all_to_all | solution.py:17
  19.5 11.8 %all-to-all-start.1 = ((bf16[8,1,9]{2,1,0:T(2,128)(2,1)}), bf16[8,1,9]{2,1,0:T(2,128)(2,1)S(1)}, u32[]{:S(2)}, u32[]{:S(2)}) async-start(bf16[8,1,9]{2,1,0:T(2,128)(2,1)} %copy.31), calls=%async_computation.1 | async-start | bytes 8192 | tf_op jit(solution)/shard_map/all_to_all | solution.py:45
  31.3 15.6 %all-to-all-start.2 = ((bf16[8,9,2048]{2,1,0:T(8,128)(2,1)}), bf16[8,9,2048]{2,1,0:T(8,128)(2,1)S(1)}, u32[]{:S(2)}, u32[]{:S(2)}) async-start(bf16[8,9,2048]{2,1,0:T(8,128)(2,1)} %convolution_convert_fusion), calls=%async_computation.2 | async-start | bytes 1048576 | tf_op jit(solution)/shard_map/all_to_all | solution.py:44
  47.1 26.5 %copy-start.4 = (s32[32,2]{0,1:T(2,128)S(1)}, s32[32,2]{0,1:T(2,128)}, u32[]{:S(2)}) copy-start(s32[32,2]{0,1:T(2,128)} %param.8) | copy-start | bytes 772
  63.3 10.1 %all-to-all-start.3 = ((f32[8,1,9]{2,1,0:T(1,128)}), f32[8,1,9]{2,1,0:T(1,128)S(1)}, u32[]{:S(2)}, u32[]{:S(2)}) async-start(f32[8,1,9]{2,1,0:T(1,128)} %bitcast.12), calls=%async_computation.3 | async-start | bytes 8192 | tf_op jit(solution)/shard_map/all_to_all | solution.py:58
  67.0 223.4 %all-reduce.2.cloned.1.call-start = ((), (), s32[]{:S(2)}) async-start(), calls=%async_computation.5 | async-start | bytes 131072 | tf_op jit(solution)/shard_map/psum | solution.py:72
  74.5 275.8 %reduce-scatter.4.cloned.1.call-start = ((), (), s32[]{:S(2)}) async-start(), calls=%async_computation.6 | async-start | bytes 39321600
  129.0 0.8 copy-start.3
  129.8 221.9 %copy-start.1 = (bf16[32,2048]{1,0:T(8,128)(2,1)S(1)}, bf16[32,2048]{1,0:T(8,128)(2,1)}, u32[]{:S(2)}) copy-start(bf16[32,2048]{1,0:T(8,128)(2,1)} %param.11) | copy-start | bytes 393220
Sparse Core Ops, SparseCore 0:
  74.6 215.7 all-reduce.1
Sparse Core Ops, SparseCore 1:
  129.2 221.0 reduce-scatter.3
where the time goes:
time: 361 us; the launch traced here: 359 us
  waiting for transfers between devices  245 us (68%)
  local copies, waits for them, and re-layouts  45.8 us (13%)
  matrix products  33.3 us (9%)
  starting transfers between devices  17 us (5%)
  between operations  15.6 us (4%)
    psum x1, waiting for transfers between devices, per_device(): router_grad = lax.psum(router_local, ('dp', 'expert', 'tensor'))  160 us
    unnamed x3, waiting for transfers between devices  59.9 us
    unnamed x14, local copies, waits for them, and re-layouts  43.7 us
    dot_general x1, matrix products, per_device(): lax.dot_general(recv_grad, down_weight, (((1,), (1,)), ((), ())), preferr...  15.5 us
    dot_general x1, matrix products, per_device(): lax.dot_general(hidden_rows, gated_grad, (((0,), (0,)), ((), ())), prefer...  13.9 us
    all_to_all x1, waiting for transfers between devices, per_device(): lax.all_to_all(send_grad, ('expert', 'tensor'), split_axis=0, concat_axis...  12 us
  transfers between devices with their start and end apart: 6, of which 6 were waited for; matrix products, arithmetic and copies ran while one was open for 16% of the time, Pallas kernels for 0%

commit v1 on v0

--- a/solution.py
+++ b/solution.py
@@ -69,7 +69,7 @@
     router_local = jnp.dot(
         full_input.astype(jnp.float32).T, logit_grad, precision=lax.Precision.HIGHEST
     )
-    router_grad = lax.psum(router_local, ("dp", "expert", "tensor"))
+    router_grad = lax.psum(lax.psum(router_local, "dp"), ("expert", "tensor"))
     weight_sum = lax.psum_scatter(
         lax.dot_general(
             hidden_rows, gated_grad, (((0,), (0,)), ((), ())), preferred_element_type=jnp.float32

time: 361 us -> 411 us (1.14)
  waiting for transfers between devices: 245 us -> 292 us
  blocking collectives: 0 us -> 9.96 us
    unnamed x3 -> x4, waiting for transfers between devices: 59.9 us -> 227 us
    psum x1 -> x2, waiting for transfers between devices: 160 us -> 45 us  [per_device(): router_grad = lax.psum(lax.psum(router_local, 'dp'), ('expert', 'tensor'))]
    all_to_all x0 -> x1, blocking collectives: none -> 9.96 us  [per_device(): lax.all_to_all(gate_partial, ('expert', 'tensor'), split_axis=0, concat_a...]
    all_to_all x1 -> x0, waiting for transfers between devices: 6.07 us -> none  [per_device(): lax.all_to_all(gate_partial, ('expert', 'tensor'), split_axis=0, concat_a...]
  transfers between devices with their start and end apart: 6 -> 6, of which waited for: 6 -> 6; matrix products, arithmetic and copies ran while one was open for 16% -> 14% of each run, Pallas kernels for 0% -> 0%
where the time goes in v1:
time: 411 us; the launch traced here: 410 us
  waiting for transfers between devices  292 us (71%)
  local copies, waits for them, and re-layouts  45.3 us (11%)
  matrix products  33.2 us (8%)
  between operations  13.9 us (3%)
  starting transfers between devices  13.4 us (3%)
  blocking collectives  9.96 us (2%)
    unnamed x4, waiting for transfers between devices  227 us
    psum x2, waiting for transfers between devices, per_device(): router_grad = lax.psum(lax.psum(router_local, 'dp'), ('expert', 'tensor'))  45 us
    unnamed x14, local copies, waits for them, and re-layouts  43.8 us
    dot_general x1, matrix products, per_device(): lax.dot_general(recv_grad, down_weight, (((1,), (1,)), ((), ())), preferr...  15.5 us
    dot_general x1, matrix products, per_device(): lax.dot_general(hidden_rows, gated_grad, (((0,), (0,)), ((), ())), prefer...  13.8 us
    all_to_all x1, waiting for transfers between devices, per_device(): lax.all_to_all(send_grad, ('expert', 'tensor'), split_axis=0, concat_axis...  12 us
    all_to_all x1, blocking collectives, per_device(): lax.all_to_all(gate_partial, ('expert', 'tensor'), split_axis=0, concat_a...  9.96 us
  transfers between devices with their start and end apart: 6, of which 6 were waited for; matrix products, arithmetic and copies ran while one was open for 14% of the time, Pallas kernels for 0%

profile of v1, /device:TPU:0, one launch (start us, length us, event | category | flops | bytes accessed | tf_op | source)
XLA Modules:
  0.0 409.6 jit_solution(14349591939113221509)
XLA Ops:
  7.2 4.4 %all-to-all-start = ((bf16[2,32,1024]{2,1,0:T(8,128)(2,1)}), bf16[2,32,1024]{2,1,0:T(8,128)(2,1)S(1)}, u32[]{:S(2)}, u32[]{:S(2)}) async-start(bf16[2,32,1024]{2,1,0:T(8,128)(2,1)} %bitcast.52), calls=%async_computation | async-start | bytes 262144 | tf_op jit(solution)/shard_map/all_to_all | solution.py:17
  11.6 0.8 copy.28
  12.3 0.7 convert_convert_fusion
  13.7 2.4 all-to-all-done
  16.1 0.9 fusion.15
  17.0 0.7 multiply_reduce_fusion.3
  17.8 0.2 fusion.2
  18.1 0.6 copy.31
  18.7 5.4 %all-to-all-start.1 = ((bf16[8,1,9]{2,1,0:T(2,128)(2,1)}), bf16[8,1,9]{2,1,0:T(2,128)(2,1)S(1)}, u32[]{:S(2)}, u32[]{:S(2)}) async-start(bf16[8,1,9]{2,1,0:T(2,128)(2,1)} %copy.31), calls=%async_computation.1 | async-start | bytes 8192 | tf_op jit(solution)/shard_map/all_to_all | solution.py:45
  24.1 1.1 convolution_convert_fusion
  25.2 5.3 %all-to-all-done.1 = bf16[8,1,9]{2,1,0:T(2,128)(2,1)S(1)} async-done(((bf16[8,1,9]{2,1,0:T(2,128)(2,1)}), bf16[8,1,9]{2,1,0:T(2,128)(2,1)S(1)}, u32[]{:S(2)}, u32[]{:S(2)}) %all-to-all-start.1) | async-done | bytes 176 | tf_op jit(solution)/shard_map/all_to_all | solution.py:45
  30.5 3.5 all-to-all-start.2
  34.1 12.0 %all-to-all-done.2 = bf16[8,9,2048]{2,1,0:T(8,128)(2,1)S(1)} async-done(((bf16[8,9,2048]{2,1,0:T(8,128)(2,1)}), bf16[8,9,2048]{2,1,0:T(8,128)(2,1)S(1)}, u32[]{:S(2)}, u32[]{:S(2)}) %all-to-all-start.2) | async-done | bytes 294944 | tf_op jit(solution)/shard_map/all_to_all | solution.py:44
  46.3 15.5 %multiply_reduce_fusion = (f32[72]{0:T(128)S(1)}, bf16[1,72,7680]{2,1,0:T(8,128)(2,1)}) fusion(bf16[1,72,7680]{2,1,0:T(8,128)(2,1)S(1)} %copy-done.2, f32[72]{0:T(128)S(1)} %reshape.65, bf16[72,2048]{1,0:T(8,128)(2,1)S(1)} %reshape.63, bf16[7680,2048]{1,0:T(8,128)(2,1)} %param.9), kind=kOutput, calls=%fused_computation.4 | convolution fusion | flops 2267688960 | bytes 33964608 | tf_op jit(solution)/shard_map/dot_general | solution.py:51
  61.9 10.0 %all_to_all.42 = f32[8,1,9]{2,1,0:T(1,128)S(1)} all-to-all(f32[8,1,9]{2,1,0:T(1,128)S(1)} %bitcast.54), channel_id=1, replica_groups=mesh['dp'=4,'expert'=4,'tensor'=2] {'expert','tensor'}, dimensions={0} | all-to-all | bytes 576 | tf_op jit(solution)/shard_map/all_to_all | solution.py:58
  72.1 0.8 convolution_bitcast_fusion
  73.2 28.6 %all-reduce.3.cloned.1.call-done = f32[2048,8]{0,1:T(8,128)} async-done(((f32[2048,8]{0,1:T(8,128)}), f32[2048,8]{0,1:T(8,128)}) %all-reduce.3.cloned.1.call-update) | async-done | bytes 65552 | tf_op jit(solution)/shard_map/psum | solution.py:72
  101.9 13.8 %convert_bitcast_fusion = bf16[7680,2048]{0,1:T(8,128)(2,1)} fusion(bf16[72,2048]{1,0:T(8,128)(2,1)S(1)} %convert_element_type.93, bf16[1,72,7680]{2,1,0:T(8,128)(2,1)S(1)} %copy-done.2), kind=kOutput, calls=%fused_computation | convolution fusion | flops 2280652800 | bytes 32858112 | tf_op jit(solution)/shard_map/dot_general | solution.py:74
  115.7 40.7 %copy.43 = bf16[7680,2048]{1,0:T(8,128)(2,1)} copy(bf16[7680,2048]{0,1:T(8,128)(2,1)} %convert_bitcast_fusion) | data formatting | bytes 62914560
  156.5 0.7 copy-done.3
  157.2 1.0 convolution_convert_fusion.1
  158.2 16.4 %all-reduce.5.cloned.1.call-done = f32[2048,8]{0,1:T(8,128)} async-done(((f32[2048,8]{0,1:T(8,128)}), f32[2048,8]{0,1:T(8,128)}) %all-reduce.5.cloned.1.call-update) | async-done | bytes 65552 | tf_op jit(solution)/shard_map/psum | solution.py:72
  174.6 227.0 %reduce-scatter.4.cloned.1.call-done = bf16[1920,2048]{1,0:T(8,128)(2,1)} async-done(((bf16[7680,2048]{1,0:T(8,128)(2,1)}), bf16[1920,2048]{1,0:T(8,128)(2,1)}) %reduce-scatter.4.cloned.1.call-update) | async-done | bytes 7864336
  401.6 1.5 copy.56
  (39 shorter events, 1.8 us)
Async XLA Ops:
  7.2 16.9 %copy-start = (bf16[32,2048]{1,0:T(8,128)(2,1)S(1)}, bf16[32,2048]{1,0:T(8,128)(2,1)}, u32[]{:S(2)}) copy-start(bf16[32,2048]{1,0:T(8,128)(2,1)} %param.11) | copy-start | bytes 393220
  7.2 39.1 %copy-start.2 = (bf16[1,72,7680]{2,1,0:T(8,128)(2,1)S(1)}, bf16[1,72,7680]{2,1,0:T(8,128)(2,1)}, u32[]{:S(2)}) copy-start(bf16[1,72,7680]{2,1,0:T(8,128)(2,1)} %param.10) | copy-start | bytes 3317764
  7.2 8.9 %all-to-all-start = ((bf16[2,32,1024]{2,1,0:T(8,128)(2,1)}), bf16[2,32,1024]{2,1,0:T(8,128)(2,1)S(1)}, u32[]{:S(2)}, u32[]{:S(2)}) async-start(bf16[2,32,1024]{2,1,0:T(8,128)(2,1)} %bitcast.52), calls=%async_computation | async-start | bytes 262144 | tf_op jit(solution)/shard_map/all_to_all | solution.py:17
  18.7 11.8 %all-to-all-start.1 = ((bf16[8,1,9]{2,1,0:T(2,128)(2,1)}), bf16[8,1,9]{2,1,0:T(2,128)(2,1)S(1)}, u32[]{:S(2)}, u32[]{:S(2)}) async-start(bf16[8,1,9]{2,1,0:T(2,128)(2,1)} %copy.31), calls=%async_computation.1 | async-start | bytes 8192 | tf_op jit(solution)/shard_map/all_to_all | solution.py:45
  30.5 15.6 %all-to-all-start.2 = ((bf16[8,9,2048]{2,1,0:T(8,128)(2,1)}), bf16[8,9,2048]{2,1,0:T(8,128)(2,1)S(1)}, u32[]{:S(2)}, u32[]{:S(2)}) async-start(bf16[8,9,2048]{2,1,0:T(8,128)(2,1)} %convolution_convert_fusion), calls=%async_computation.2 | async-start | bytes 1048576 | tf_op jit(solution)/shard_map/all_to_all | solution.py:44
  34.0 67.9 %all-reduce.3.cloned.1.call-start = ((), (), s32[]{:S(2)}) async-start(), calls=%async_computation.5 | async-start | bytes 131072 | tf_op jit(solution)/shard_map/psum | solution.py:72
  46.3 25.8 %copy-start.4 = (s32[32,2]{0,1:T(2,128)S(1)}, s32[32,2]{0,1:T(2,128)}, u32[]{:S(2)}) copy-start(s32[32,2]{0,1:T(2,128)} %param.8) | copy-start | bytes 772
  72.9 101.7 %all-reduce.5.cloned.1.call-start = ((), (), s32[]{:S(2)}) async-start(), calls=%async_computation.6 | async-start | bytes 131072 | tf_op jit(solution)/shard_map/psum | solution.py:72
  101.9 299.7 %reduce-scatter.4.cloned.1.call-start = ((), (), s32[]{:S(2)}) async-start(), calls=%async_computation.7 | async-start | bytes 39321600
  156.5 0.8 copy-start.3
  157.2 245.8 %copy-start.1 = (bf16[32,2048]{1,0:T(8,128)(2,1)S(1)}, bf16[32,2048]{1,0:T(8,128)(2,1)}, u32[]{:S(2)}) copy-start(bf16[32,2048]{1,0:T(8,128)(2,1)} %param.11) | copy-start | bytes 393220
Sparse Core Ops, SparseCore 0:
  73.0 28.8 all-reduce.2
  105.3 69.2 all-reduce.4
  177.7 223.7 reduce-scatter.3
